TPU v7x, 128 devices: a whole 4x4x4 slice. The times are simulated.
128 devices in a mesh: dp: 1, tp: 2 (over core), sp: 64 (over z, y, x).
Axes of the slice: x: 4, y: 4, z: 4, core: 2. Of those that a mesh axis runs over, the one named last changes fastest.
Arguments:
- hidden: bfloat16 [32, 5120], P('dp')
- lat_cache: bfloat16 [32, 16384, 512], P('dp', 'sp')
- rope_cache: bfloat16 [32, 16384, 64], P('dp', 'sp')
- positions: int32 [32], P('dp')
- w_dq: bfloat16 [5120, 1536], replicated
- gain_q: bfloat16 [1536], replicated
- w_dkv: bfloat16 [5120, 576], replicated
- gain_kv: bfloat16 [512], replicated
- w_uq: bfloat16 [1536, 128, 192], P(None, 'tp')
- w_uk: bfloat16 [512, 128, 128], P(None, 'tp')
- w_uv: bfloat16 [512, 128, 128], P(None, 'tp')
- w_out: bfloat16 [16384, 5120], P('tp')
Outputs:
- output 1: bfloat16 [32, 5120], P('dp')
- output 2: bfloat16 [32, 16384, 512], P('dp', 'sp')
- output 3: bfloat16 [32, 16384, 64], P('dp', 'sp')
All inputs are finite; a program needn't handle non-finite values.
Results may differ from a plain program's by a relative error of at most 0.00918123.
Values sent between devices are 32-bit elements.
A program may use at most 1 GiB of HBM per device.

v0:
```python
import functools
import math
import jax
import jax.numpy as jnp
from jax import lax
from jax.experimental import pallas as pl
from jax.experimental.pallas import tpu as pltpu
from jax.sharding import PartitionSpec as P

EPSILON = 1e-6
ROPE_BASE = 50000.0
YARN_MSCALE = 1.0 + 0.1 * math.log(32.0)
MASK_VALUE = -1e30
TILE = (8, 128)
HEAD_GROUP = 16
UQ_RING = 4
MIB = 2 ** 20
FRONT_VMEM = 48 * MIB
ATTEND_VMEM = 46 * MIB
TAIL_VMEM = 50 * MIB
SEND_ORDER = (2, 1, 3)
WAIT_ORDER = (1, 3, 2)
MESH = pl.DeviceIdType.MESH
NT = (((1,), (1,)), ((), ()))
f32, bf16 = jnp.float32, jnp.bfloat16

HEAD_STRIDE = (16, 4, 1)
SP_STRIDE = (1, 4, 16)
ORDERS = ((0, 1, 2), (1, 2, 0), (2, 0, 1))
UNIT_LO = (0, 5, 10)
UNIT_MID = (2, 8, 13)
UNIT_HI = (5, 10, 16)
RING = (1, 3)
RING_STEPS = (1, 2, 3)
OUT_LO = (0, 256)
OUT_HI = (256, 640)


def rope_tables(positions, rope_dim):
    half_dim = rope_dim // 2
    inv_freq = ROPE_BASE ** (-jnp.arange(half_dim).astype(jnp.float32) / half_dim)
    angles = positions.astype(jnp.float32)[:, None] * inv_freq[None, :]
    return jnp.cos(angles), jnp.sin(angles)


def front_kernel(hid_ref, gq_ref, gkv_ref, cos_ref, sin_ref, wdkv_hbm, wdq_hbm, wuk_hbm, wuq_hbm,
                 qabs_ref, qrope_ref, lnew_ref, rnew_ref, wdkv_v, wdq_v, wuk_v, wuq_v, sem_kv, sem_q, sem_k, sem_u):
    n_kv, n_q, ring = wdkv_v.shape[0], wdq_v.shape[0], wuq_v.shape[0]
    kv_cols, q_rows, part = wdkv_v.shape[2], wdq_v.shape[1], wuq_v.shape[1]
    n_parts = wuq_hbm.shape[0] // part

    def load_uq(i):
        return pltpu.make_async_copy(wuq_hbm.at[pl.ds(i * part, part)], wuq_v.at[i % ring], sem_u.at[i % ring])

    kv_loads = [pltpu.make_async_copy(wdkv_hbm.at[:, pl.ds(i * kv_cols, kv_cols)], wdkv_v.at[i], sem_kv.at[i]) for i in range(n_kv)]
    q_loads = [pltpu.make_async_copy(wdq_hbm.at[pl.ds(i * q_rows, q_rows), :], wdq_v.at[i], sem_q.at[i]) for i in range(n_q)]
    k_rows = wuk_v.shape[0] // 4
    k_loads = [pltpu.make_async_copy(wuk_hbm.at[pl.ds(i * k_rows, k_rows)], wuk_v.at[pl.ds(i * k_rows, k_rows)], sem_k.at[i]) for i in range(4)]
    uq_loads = [load_uq(i) for i in range(n_parts)]
    queue = kv_loads + q_loads + uq_loads[:2] + k_loads + uq_loads[2:]
    state = [0]

    def issue(count):
        for copy in queue[state[0]:state[0] + count]:
            copy.start()
        state[0] += count

    issue(UQ_RING)
    cos_t, sin_t = cos_ref[...], sin_ref[...]
    half = cos_t.shape[1]

    def rotate(v):
        v1, v2 = v[:, :half], v[:, half:]
        return jnp.concatenate([v1 * cos_t - v2 * sin_t, v2 * cos_t + v1 * sin_t], axis=1)

    def norm(values, gain_ref):
        v = values.astype(bf16).astype(f32)
        inv = lax.rsqrt(jnp.mean(v * v, axis=1, keepdims=True) + EPSILON)
        return (v * inv * gain_ref[...].astype(f32)).astype(bf16)

    kv = jnp.zeros((32, wdkv_v.shape[1]), f32)
    for i in range(n_kv):
        kv_loads[i].wait()
        issue(1)
        kv = kv + lax.dot_general(hid_ref[:, i * kv_cols:(i + 1) * kv_cols], wdkv_v[i], NT, preferred_element_type=f32)
    lnew_ref[...] = norm(kv[:, :512], gkv_ref)
    turned = rotate(kv[:, 512:].astype(bf16).astype(f32)).T.astype(bf16)
    for t in range(4):
        rnew_ref[t] = turned[:, t * 8:t * 8 + 8]
    h_q = jnp.zeros((32, 1536), f32)
    for i in range(n_q):
        q_loads[i].wait()
        issue(1)
        h_q = h_q + jnp.dot(hid_ref[:, i * q_rows:(i + 1) * q_rows], wdq_v[i], preferred_element_type=f32)
    cq = norm(h_q, gq_ref)

    nope, rotated = [], []
    zero = jnp.zeros((32, 128), bf16)

    def absorb(group):
        wuk = jnp.swapaxes(wuk_v[:, group * HEAD_GROUP:(group + 1) * HEAD_GROUP, :], 0, 1)
        absorbed = []
        for i in range(0, HEAD_GROUP, 2):
            a, b = nope[group * HEAD_GROUP + i], nope[group * HEAD_GROUP + i + 1]
            pair = jnp.concatenate([jnp.concatenate([a, zero], axis=1), jnp.concatenate([zero, b], axis=1)], axis=0)
            both = lax.dot_general(pair, jnp.concatenate([wuk[i], wuk[i + 1]], axis=1), NT, preferred_element_type=f32)
            absorbed += [both[:32], both[32:]]
        where = slice(group * HEAD_GROUP, (group + 1) * HEAD_GROUP)
        qabs_ref[:, where, :] = jnp.swapaxes(jnp.stack(absorbed), 0, 1).astype(bf16)
        qrope_ref[:, where, :] = jnp.swapaxes(jnp.stack(rotated[where]), 0, 1).astype(bf16)

    per_group = HEAD_GROUP // part
    for i in range(n_parts):
        uq_loads[i].wait()
        w = wuq_v[i % ring].reshape(part * 192, 1536)
        q4 = lax.dot_general(cq, w, NT, preferred_element_type=f32).astype(bf16)
        for j in range(part):
            q = q4[:, j * 192:j * 192 + 192]
            nope.append(q[:, :128])
            rotated.append(rotate(q[:, 128:].astype(f32)))
        issue(1)
        if i == 1:
            for copy in k_loads:
                copy.wait()
                issue(1)
        if i % per_group == per_group - 1:
            absorb(i // per_group)


def front(hidden, gain_q, gain_kv, cos_t, sin_t, w_dkv, w_dq, w_uk, w_uq):
    heads = w_uq.shape[1]
    vmem = pl.BlockSpec(memory_space=pltpu.VMEM)
    hbm = pl.BlockSpec(memory_space=pltpu.HBM)
    dma = pltpu.SemaphoreType.DMA
    shape = jax.ShapeDtypeStruct
    return pl.pallas_call(
        front_kernel,
        out_shape=(shape((32, heads, 512), bf16), shape((32, heads, 64), bf16), shape((32, 512), bf16), shape((4, 64, 8), bf16)),
        in_specs=[vmem] * 5 + [hbm] * 4,
        out_specs=[vmem] * 4,
        scratch_shapes=[
            pltpu.VMEM((4, 576, 1280), bf16),
            pltpu.VMEM((5, 1024, 1536), bf16),
            pltpu.VMEM((512, heads, 128), bf16),
            pltpu.VMEM((UQ_RING, 4, 192, 1536), bf16),
            dma((4,)), dma((5,)), dma((4,)), dma((UQ_RING,)),
        ],
        compiler_params=pltpu.CompilerParams(vmem_limit_bytes=FRONT_VMEM),
        name='front',
    )(hidden, gain_q.reshape(1, -1), gain_kv.reshape(1, -1), cos_t, sin_t, w_dkv.T, w_dq, w_uk, w_uq.transpose(1, 2, 0))


def attend_kernel(base_ref, pos_ref, qabs_ref, qrope_ref, lat_ref, rope_ref, lnew_ref, rnew_ref,
                  lat_out, rope_out, u_ref, st_ref, s_buf, w_buf, *, scale):
    tile = pl.program_id(0)
    base = base_ref[0]
    lane256 = lax.broadcasted_iota(jnp.int32, (64, 256), 1)
    lane128 = lax.broadcasted_iota(jnp.int32, (64, 128), 1)
    row16 = lax.broadcasted_iota(jnp.int32, (16, 512), 0)
    lat_out[...] = lat_ref[...]
    slots = [pos_ref[tile * 8 + b] - base for b in range(8)]
    for b in range(8):
        slot = slots[b]
        group = jnp.clip(slot // 16, 0, 15) * 16
        rows = pl.ds(pl.multiple_of(group, 16), 16)
        new = jnp.broadcast_to(lnew_ref[b:b + 1, :].astype(f32), (16, 512))
        lat_out[b, rows, :] = jnp.where(row16 == slot - group, new, lat_ref[b, rows, :].astype(f32)).astype(bf16)
        rope_out[b] = jnp.where(lane256 == slot, rnew_ref[0, :, b:b + 1].astype(f32), rope_ref[b].astype(f32)).astype(bf16)
    for b in range(8):
        s = lax.dot_general(qabs_ref[tile * 8 + b], lat_out[b], NT, preferred_element_type=f32)
        s_buf[b] = s + jnp.dot(qrope_ref[tile * 8 + b], rope_out[b], preferred_element_type=f32)
    tops = jnp.zeros((64, 128), f32)
    dens = jnp.zeros((64, 128), f32)
    for b in range(8):
        s = jnp.where(lane256 <= slots[b], s_buf[b] * scale, MASK_VALUE)
        top = jnp.max(s, axis=1, keepdims=True)
        w = jnp.exp(s - top)
        den = jnp.sum(w, axis=1, keepdims=True)
        w_buf[b] = w.astype(bf16)
        tops = jnp.where(lane128 == b, top, tops)
        dens = jnp.where(lane128 == b, den, dens)
    st_ref[0] = jnp.concatenate([tops, dens], axis=0).T[:8, :]
    for b in range(8):
        u = jnp.dot(w_buf[b], lat_out[b], preferred_element_type=f32)
        for kt in range(4):
            u_ref[tile * 4 + kt, pl.ds(b, 64, stride=8), :] = u[:, kt * 128:kt * 128 + 128]


def attend(base, positions, q_abs, q_rope, lat_cache, rope_t, lat_new, rope_new, scale):
    vmem = pl.BlockSpec(memory_space=pltpu.VMEM)
    smem = pl.BlockSpec(memory_space=pltpu.SMEM)
    first = lambda t: (t, 0, 0)
    return pl.pallas_call(
        functools.partial(attend_kernel, scale=scale),
        grid=(4,),
        out_shape=(jax.ShapeDtypeStruct((32, 256, 512), bf16), jax.ShapeDtypeStruct((32, 64, 256), bf16),
                   jax.ShapeDtypeStruct((16, 512, 128), f32), jax.ShapeDtypeStruct((4, 8, 128), f32)),
        in_specs=[smem, smem,
                  vmem, vmem,
                  pl.BlockSpec((8, 256, 512), first), pl.BlockSpec((8, 64, 256), first),
                  pl.BlockSpec((8, 512), lambda t: (t, 0)), pl.BlockSpec((1, 64, 8), first)],
        out_specs=[pl.BlockSpec((8, 256, 512), first), pl.BlockSpec((8, 64, 256), first),
                   vmem, pl.BlockSpec((1, 8, 128), first)],
        scratch_shapes=[pltpu.VMEM((8, 64, 256), f32), pltpu.VMEM((8, 64, 256), bf16)],
        compiler_params=pltpu.CompilerParams(vmem_limit_bytes=ATTEND_VMEM),
        name='attend',
    )(base, positions, q_abs, q_rope, lat_cache, rope_t, lat_new, rope_new)


def tail_kernel(u_ref, st_ref, wuv_ref, wout_ref, out_ref,
                relay, passed, r1, v1, r2, v2, r3, s1, s2, q0, q1, q2, q3,
                wuv_v, wuv_h, wout_v, y_buf, y_in, t1, t2, p1, p2, zbuf, g_buf,
                send_sem, recv_sem, load_sem):
    sp = lax.axis_index('sp')
    tp = lax.axis_index('tp')
    coord = (lax.rem(sp, 4), lax.rem(sp // 4, 4), sp // 16)
    x, y, z = coord
    head = x * 16 + y * 4 + z
    group = pl.multiple_of((head // 8) * 8, 8)

    load_uv = pltpu.make_async_copy(wuv_ref.at[:, pl.ds(group, 8), :], wuv_v, load_sem.at[0])
    load_uv.start()
    load_out = pltpu.make_async_copy(wout_ref.at[pl.ds(pl.multiple_of(head * 128, 128), 128), :], wout_v, load_sem.at[1])
    load_out.start()

    def peer_coord(axis, step):
        return lax.rem(coord[axis] + step, 4)

    def peer_id(axis, step):
        return {'sp': sp + (peer_coord(axis, step) - coord[axis]) * SP_STRIDE[axis]}

    barrier = pltpu.get_barrier_semaphore()
    for axis in range(3):
        for step in RING_STEPS:
            pl.semaphore_signal(barrier, inc=1, device_id=peer_id(axis, step), device_id_type=MESH)
    pl.semaphore_signal(barrier, inc=1, device_id={'tp': 1 - tp}, device_id_type=MESH)
    pl.semaphore_wait(barrier, 10)

    started = []

    def send(src, dst, device):
        index = len(started)
        copy = pltpu.make_async_remote_copy(
            src_ref=src, dst_ref=dst, send_sem=send_sem.at[index], recv_sem=recv_sem.at[index],
            device_id=device, device_id_type=MESH)
        copy.start()
        started.append(copy)
        return copy

    lane = lax.broadcasted_iota(jnp.int32, (2, 8, 128), 2)

    def merge_stats(stats, offset, turn_result=True):
        top = functools.reduce(jnp.maximum, stats)
        shift = lax.rem(128 - offset, 128)
        factors = [jnp.exp(s - top) for s in stats]
        den = sum(f * pltpu.roll(s, 64, 2) for f, s in zip(factors, stats))
        merged = jnp.where(lane < 64, top, pltpu.roll(den, 64, 2))
        if turn_result:
            merged = pltpu.roll(merged, shift, 2)
        return merged, [pltpu.roll(f, shift, 2) for f in factors]

    def spread(factor, lane_index):
        return jnp.broadcast_to(factor[:, lane_index:lane_index + 1], (8, 128))

    pending = {}

    def block(axis, position, lo, hi):
        sel = [slice(None)] * 3
        sel[axis] = position
        return u_ref.at[(pl.ds(lo, hi - lo),) + tuple(sel)]

    for colour in range(3):
        axis = ORDERS[colour][0]
        ends = (UNIT_LO[colour], UNIT_MID[colour], UNIT_HI[colour])
        far = peer_coord(axis, 2)
        for side, step in enumerate(RING):
            peer, near = peer_id(axis, step), peer_coord(axis, step)
            lo, hi = ends[side], ends[side + 1]
            pending[colour, side, 'stats'] = send(st_ref.at[pl.ds(colour, 2)], q1.at[colour, side], peer)
            pending[colour, side, 'relay'] = send(block(axis, far, lo, hi), relay.at[pl.ds(lo, hi - lo)], peer)
            lo, hi = ends[1 - side], ends[2 - side]
            pending[colour, side, 'near'] = send(block(axis, near, lo, hi), r1.at[0, pl.ds(lo, hi - lo)], peer)

    def ring_sum(colour, lo, hi, position, factors, arrays, store):
        axis = ORDERS[colour][0]
        first, second = [a for a in range(3) if a != axis]
        for i in range(4):
            for j in range(4):
                where = HEAD_STRIDE[first] * i + HEAD_STRIDE[second] * j
                at = [None] * 3
                at[axis], at[first], at[second] = position, i, j
                for bt in range(lo // 4, (hi - 1) // 4 + 1):
                    fb = [spread(f[bt - colour], where) for f in factors]
                    for unit in range(max(lo, bt * 4), min(hi, bt * 4 + 4)):
                        total = fb[0] * u_ref[unit, at[0], at[1], at[2]]
                        for f, array in zip(fb[1:], arrays):
                            total = total + f * array[unit, i, j]
                        store[unit, i, j] = total

    for colour in range(3):
        axis = ORDERS[colour][0]
        ends = (UNIT_LO[colour], UNIT_MID[colour], UNIT_HI[colour])
        for side, step in enumerate(RING):
            pending[colour, side, 'stats'].wait_recv()
            lo, hi = ends[side], ends[side + 1]
            peer, near = peer_id(axis, step), peer_coord(axis, step)
            pending[colour, side, 'relay'].wait_recv()
            merged, factors = merge_stats([st_ref[pl.ds(colour, 2)], q1[colour, side]], near * HEAD_STRIDE[axis], False)
            q0[colour, side] = merged
            ring_sum(colour, lo, hi, near, factors, [relay], passed)
            pending[colour, side, 'sum stats'] = send(q0.at[colour, side], q1.at[colour, 2 + side], peer)
            pending[colour, side, 'sum'] = send(passed.at[pl.ds(lo, hi - lo)], r1.at[1, pl.ds(lo, hi - lo)], peer)

    load_uv.wait()
    pick = lax.broadcasted_iota(jnp.int32, (64, 8, 128), 1) == lax.rem(head, 8)

    def pick_rows(i, carry):
        rows = pl.ds(pl.multiple_of(i * 64, 64), 64)
        wuv_h[rows, :] = jnp.sum(jnp.where(pick, wuv_v[rows].astype(f32), 0.0), axis=1).astype(bf16)
        return carry

    lax.fori_loop(0, 8, pick_rows, 0)

    for colour in range(3):
        order = ORDERS[colour]
        axis, axis2 = order[:2]
        lo, hi = UNIT_LO[colour], UNIT_HI[colour]
        ends = (lo, UNIT_MID[colour], hi)
        first, second = [a for a in range(3) if a != axis]
        for side in range(2):
            pending[colour, 1 - side, 'near'].wait_recv()
            pending[colour, side, 'sum stats'].wait_recv()
            pending[colour, side, 'sum'].wait_recv()
            stats = [st_ref[pl.ds(colour, 2)], q1[colour, 1 - side], q1[colour, 2 + side]]
            merged, factors = merge_stats(stats, coord[axis] * HEAD_STRIDE[axis])
            ring_sum(colour, ends[side], ends[side + 1], coord[axis], factors, [r1.at[0], r1.at[1]], v1)
        s1[colour] = merged
        for step in SEND_ORDER:
            pc = peer_coord(axis2, step)
            sel = (pc, slice(None)) if axis2 == first else (slice(None), pc)
            a = send(v1.at[(pl.ds(lo, hi - lo),) + sel], r2.at[step - 1, pl.ds(lo, hi - lo)], peer_id(axis2, step))
            b = send(s1.at[colour], q2.at[colour, step - 1], peer_id(axis2, step))
            pending[colour, step] = (a, b)

    for colour in range(3):
        order = ORDERS[colour]
        axis, axis2, axis3 = order
        lo, hi = UNIT_LO[colour], UNIT_HI[colour]
        first, second = [a for a in range(3) if a != axis]
        for step in WAIT_ORDER:
            for copy in pending[colour, step]:
                copy.wait_recv()
        stats = [s1[colour]] + [q2[colour, i] for i in range(3)]
        merged, factors = merge_stats(stats, coord[axis2] * HEAD_STRIDE[axis2])
        s2[colour] = merged
        for i in range(4):
            at = (coord[axis2], i) if axis2 == first else (i, coord[axis2])
            for bt in range(lo // 4, (hi - 1) // 4 + 1):
                fb = [spread(f[bt - colour], HEAD_STRIDE[axis3] * i) for f in factors]
                for unit in range(max(lo, bt * 4), min(hi, bt * 4 + 4)):
                    total = fb[0] * v1[unit, at[0], at[1]]
                    for k in range(3):
                        total = total + fb[k + 1] * r2[k, unit, i]
                    v2[unit, i] = total
        for step in SEND_ORDER:
            a = send(v2.at[pl.ds(lo, hi - lo), peer_coord(axis3, step)], r3.at[step - 1, pl.ds(lo, hi - lo)], peer_id(axis3, step))
            b = send(s2.at[colour], q3.at[colour, step - 1], peer_id(axis3, step))
            pending[colour, step] = (a, b)

    units = [None] * 16
    den = [None] * 16
    for colour in range(3):
        axis3 = ORDERS[colour][2]
        lo, hi = UNIT_LO[colour], UNIT_HI[colour]
        for step in WAIT_ORDER:
            for copy in pending[colour, step]:
                copy.wait_recv()
        stats = [s2[colour]] + [q3[colour, i] for i in range(3)]
        merged, factors = merge_stats(stats, coord[axis3] * HEAD_STRIDE[axis3])
        for bt in range(lo // 4, (hi - 1) // 4 + 1):
            fb = [spread(f[bt - colour], 0) for f in factors]
            dn = spread(merged[bt - colour], 64)
            for unit in range(max(lo, bt * 4), min(hi, bt * 4 + 4)):
                total = fb[0] * v2[unit, coord[axis3]]
                for k in range(3):
                    total = total + fb[k + 1] * r3[k, unit]
                units[unit] = total / dn
    o_lat = jnp.concatenate(
        [jnp.concatenate([units[bt * 4 + kt] for kt in range(4)], axis=1) for bt in range(4)], axis=0).astype(jnp.bfloat16)
    o_head = jnp.dot(o_lat, wuv_h[...], preferred_element_type=jnp.float32).astype(jnp.bfloat16)
    load_out.wait()
    for half in range(2):
        for cg in range(4):
            base = half * 2560 + cg * 640
            part = jnp.dot(o_head, wout_v[:, base:base + 640], preferred_element_type=jnp.float32)
            y_buf[half, :, cg] = part.reshape(4, 8, 640)

    pair = send(y_buf.at[1 - tp], y_in, {'tp': 1 - tp})
    pair.wait_recv()
    y_in[...] = y_in[...] + y_buf[tp]

    for colour in range(2):
        cols = pl.ds(OUT_LO[colour], OUT_HI[colour] - OUT_LO[colour])
        axis = colour
        for step in SEND_ORDER:
            pc = peer_coord(axis, step)
            src = y_in.at[pc, :, :, cols] if axis == 0 else y_in.at[:, pc, :, cols]
            pending[colour, step] = send(src, t1.at[step - 1, :, :, cols], peer_id(axis, step))
    for colour in range(2):
        cols = pl.ds(OUT_LO[colour], OUT_HI[colour] - OUT_LO[colour])
        axis, axis2 = colour, 1 - colour
        for step in WAIT_ORDER:
            pending[colour, step].wait_recv()
        for i in range(4):
            own = y_in[x, i, :, cols] if axis == 0 else y_in[i, y, :, cols]
            p1[i, :, cols] = own + sum(t1[k, i, :, cols] for k in range(3))
        for step in SEND_ORDER:
            pending[colour, step] = send(
                p1.at[peer_coord(axis2, step), :, cols], t2.at[step - 1, :, cols], peer_id(axis2, step))
    for colour in range(2):
        cols = pl.ds(OUT_LO[colour], OUT_HI[colour] - OUT_LO[colour])
        axis2 = 1 - colour
        for step in WAIT_ORDER:
            pending[colour, step].wait_recv()
        p2[:, cols] = p1[coord[axis2], :, cols] + sum(t2[k, :, cols] for k in range(3))

    for step in SEND_ORDER:
        pending[0, step] = send(p2, zbuf.at[z], peer_id(2, step))
    zbuf[z] = p2[...]
    for step in WAIT_ORDER:
        pending[0, step].wait_recv()
    g_buf[tp, x, y] = (zbuf[0] + zbuf[1]) + (zbuf[2] + zbuf[3])

    for colour in range(2):
        cols = pl.ds(OUT_LO[colour], OUT_HI[colour] - OUT_LO[colour])
        axis2 = 1 - colour
        mine = g_buf.at[tp, x, y, :, cols]
        for step in SEND_ORDER:
            pending[colour, step] = send(mine, mine, peer_id(axis2, step))
    for colour in range(2):
        cols = pl.ds(OUT_LO[colour], OUT_HI[colour] - OUT_LO[colour])
        axis = colour
        for step in WAIT_ORDER:
            pending[colour, step].wait_recv()
        mine = g_buf.at[tp, x, :, :, cols] if axis == 0 else g_buf.at[tp, :, y, :, cols]
        for step in SEND_ORDER:
            pending[colour, step] = send(mine, mine, peer_id(axis, step))
    for colour in range(2):
        for step in WAIT_ORDER:
            pending[colour, step].wait_recv()
    pair = send(g_buf.at[tp], g_buf.at[tp], {'tp': 1 - tp})
    pair.wait_recv()
    for half in range(2):
        for cg in range(4):
            base = half * 2560 + cg * 640
            out_ref[:, base:base + 640] = g_buf[half, :, cg].reshape(32, 640)
    for copy in started:
        copy.wait_send()


N_SENDS = 95


def tail(u_parts, stats, w_uv, w_out):
    parts = u_parts.shape[:3]
    cols = (8, 640)
    grid = parts[1:]
    vmem = pl.BlockSpec(memory_space=pltpu.VMEM)
    hbm = pl.BlockSpec(memory_space=pltpu.HBM)
    return pl.pallas_call(
        tail_kernel,
        out_shape=jax.ShapeDtypeStruct((32, 5120), f32),
        in_specs=[vmem, vmem, hbm, hbm],
        out_specs=vmem,
        scratch_shapes=[
            pltpu.VMEM(parts + TILE, f32),
            pltpu.VMEM(parts + TILE, f32),
            pltpu.VMEM((2,) + parts + TILE, f32),
            pltpu.VMEM(parts + TILE, f32),
            pltpu.VMEM((3,) + parts[:2] + TILE, f32),
            pltpu.VMEM(parts[:2] + TILE, f32),
            pltpu.VMEM((3,) + parts[:1] + TILE, f32),
            pltpu.VMEM((3, 2) + TILE, f32),
            pltpu.VMEM((3, 2) + TILE, f32),
            pltpu.VMEM((3, 2, 2) + TILE, f32),
            pltpu.VMEM((3, 4, 2) + TILE, f32),
            pltpu.VMEM((3, 3, 2) + TILE, f32),
            pltpu.VMEM((3, 3, 2) + TILE, f32),
            pltpu.VMEM((512,) + TILE, bf16),
            pltpu.VMEM((512, 128), bf16),
            pltpu.VMEM((128, 5120), bf16),
            pltpu.VMEM((2,) + grid + cols, f32),
            pltpu.VMEM(grid + cols, f32),
            pltpu.VMEM((3, 4) + cols, f32),
            pltpu.VMEM((3,) + cols, f32),
            pltpu.VMEM((4,) + cols, f32),
            pltpu.VMEM(cols, f32),
            pltpu.VMEM((4,) + cols, f32),
            pltpu.VMEM((2,) + grid + cols, f32),
            pltpu.SemaphoreType.DMA((N_SENDS,)),
            pltpu.SemaphoreType.DMA((N_SENDS,)),
            pltpu.SemaphoreType.DMA((2,)),
        ],
        compiler_params=pltpu.CompilerParams(collective_id=0, has_side_effects=True, vmem_limit_bytes=TAIL_VMEM),
        name='tail',
    )(u_parts, stats, w_uv, w_out)


def solution(mesh):
    row_spec = P('dp', None)
    cache_spec = P('dp', 'sp', None)
    head_spec = P(None, 'tp', None)
    in_specs = (row_spec, cache_spec, cache_spec, P('dp'), P(), P(), P(), P(), head_spec, head_spec, head_spec, P('tp', None))
    out_specs = (row_spec, cache_spec, cache_spec)

    def local_step(hidden, lat_cache, rope_cache, positions, w_dq, gain_q, w_dkv, gain_kv, w_uq, w_uk, w_uv, w_out):
        seq_local = lat_cache.shape[1]
        score_scale = YARN_MSCALE ** 2 / math.sqrt(w_uq.shape[2])
        cos_t, sin_t = rope_tables(positions, rope_cache.shape[2])
        q_abs, q_rope, lat_new, rope_new = front(hidden, gain_q, gain_kv, cos_t, sin_t, w_dkv, w_dq, w_uk, w_uq)
        base = (lax.axis_index('sp') * seq_local).reshape(1)
        lat_all, rope_all, u_parts, stats = attend(
            base, positions, q_abs, q_rope, lat_cache, rope_cache.transpose(0, 2, 1), lat_new, rope_new, score_scale)
        u_parts = u_parts.reshape(16, 4, 4, 4, 8, 128)
        attn_out = tail(u_parts, stats, w_uv, w_out)
        out = (hidden.astype(f32) + attn_out).astype(bf16)
        return out, lat_all, rope_all.transpose(0, 2, 1)

    return jax.shard_map(local_step, mesh=mesh, in_specs=in_specs, out_specs=out_specs, check_vma=False)
```

profile of v0, /device:TPU:1, one launch (start us, length us, event | category | flops | bytes accessed | tf_op | source)
XLA Modules:
  0.0 106.9 jit_solution(3019123135380269037)
XLA Ops:
  0.6 0.7 convert_element_type.17
  1.3 0.7 reshape.28.gkv_ref
  2.0 0.7 reshape.27.gq_ref
  2.7 0.1 multiply_sine_fusion
  2.8 0.0 copy-start.1
  2.8 1.0 copy-done.1
  3.8 0.0 copy-start.3
  3.8 0.0 copy-start.4
  3.8 32.2 %front.1 = (bf16[32,64,512]{2,1,0:T(8,128)(2,1)S(1)}, bf16[32,64,64]{2,1,0:T(8,128)(2,1)S(1)}, bf16[32,512]{1,0:T(8,128)(2,1)S(1)}, bf16[4,64,8]{2,1,0:T(8,128)(2,1)S(1)}) custom-call(bf16[32,5120]{1,0:T(8,128)(2,1)S(1)} %copy-done.1, bf16[1,1536]{1,0:T(2,128)(2,1)S(1)} %reshape.27.gq_ref, bf16[1,512]{1,0:T(2,128)(2,1)S(1)} %reshape.28.gkv_ref, ...), custom_call_target="tpu_custom_call" | custom-call | tf_op jit(solution)/shard_map/front/pallas_call | solution.py:136
  36.0 0.0 copy-done.3
  36.0 0.0 copy-done.4
  36.0 8.5 %attend.1 = (bf16[32,256,512]{2,1,0:T(8,128)(2,1)}, bf16[32,64,256]{2,1,0:T(8,128)(2,1)}, f32[16,512,128]{2,1,0:T(8,128)S(1)}, f32[4,8,128]{2,1,0:T(8,128)S(1)}) custom-call(s32[1]{0:T(128)} %bitcast.base_ref, s32[32]{0:T(128)S(1)} %copy-done.4, bf16[32,64,512]{2,1,0:T(8,128)(2,1)S(1)} %get-tuple-element.11.qabs_ref, ...), custom_call_target="tpu_custom_call" | custom-call | tf_op jit(solution)/shard_map/attend/pallas_call | solution.py:193
  44.5 0.0 copy-start
  44.5 1.9 %copy-done = f32[16,512,128]{2,1,0:T(8,128)} copy-done((f32[16,512,128]{2,1,0:T(8,128)}, f32[16,512,128]{2,1,0:T(8,128)S(1)}, u32[]{:S(2)}) %copy-start) | copy-done | bytes 4194328
  46.4 0.0 copy-start.2
  46.4 59.7 %tail.1 = f32[32,5120]{1,0:T(8,128)S(1)} custom-call(f32[16,4,4,4,8,128]{5,4,3,2,1,0:T(8,128)} %bitcast.6, f32[4,8,128]{2,1,0:T(8,128)S(1)} %get-tuple-element.16.st_ref, bf16[512,64,128]{2,1,0:T(8,128)(2,1)} %wuv_ref.1, bf16[8192,5120]{1,0:T(8,128)(2,1)} %wout_ref.1), custom_call_target="tpu_custom_call" | custom-call | tf_op jit(solution)/shard_map/tail/pallas_call | solution.py:470
  106.1 0.0 copy-done.2
  106.1 0.8 add_convert_fusion
  (1 shorter events, 0.0 us)
Async XLA Ops:
  2.8 1.0 copy-start.1
  3.8 32.2 %copy-start.3 = (bf16[32,256,64]{1,2,0:T(8,128)(2,1)S(1)}, bf16[32,256,64]{1,2,0:T(8,128)(2,1)}, u32[]{:S(2)}) copy-start(bf16[32,256,64]{1,2,0:T(8,128)(2,1)} %param.14) | copy-start | bytes 3145732
  3.8 32.2 %copy-start.4 = (s32[32]{0:T(128)S(1)}, s32[32]{0:T(128)}, u32[]{:S(2)}) copy-start(s32[32]{0:T(128)} %pos_ref.1) | copy-start | bytes 388
  44.5 1.9 %copy-start = (f32[16,512,128]{2,1,0:T(8,128)}, f32[16,512,128]{2,1,0:T(8,128)S(1)}, u32[]{:S(2)}) copy-start(f32[16,512,128]{2,1,0:T(8,128)S(1)} %get-tuple-element.15) | copy-start | bytes 12582916
  46.4 59.7 %copy-start.2 = (bf16[32,5120]{1,0:T(8,128)(2,1)S(1)}, bf16[32,5120]{1,0:T(8,128)(2,1)}, u32[]{:S(2)}) copy-start(bf16[32,5120]{1,0:T(8,128)(2,1)} %hid_ref.1) | copy-start | bytes 983044
where the time goes:
time: 107 us
  Pallas kernels  100 us (93%)
  local copies, waits for them, and re-layouts  4.3 us (4%)
  other arithmetic  1.59 us (1%)
    pallas_call x1, Pallas kernels, tail(): pl.pallas_call(tail_kernel, out_shape=jax.ShapeDtypeStruct((32, 5120), f3...  59.7 us
    pallas_call x1, Pallas kernels, front(): pl.pallas_call(front_kernel, out_shape=(shape((32, heads, 512), bf16), sh...  32.2 us
    pallas_call x1, Pallas kernels, attend(): pl.pallas_call(functools.partial(attend_kernel, scale=scale), grid=(4,),...  8.49 us
    unnamed x10, local copies, waits for them, and re-layouts  2.92 us

commit v1 on v0

--- a/solution.py
+++ b/solution.py
@@ -17,7 +17,7 @@
 MIB = 2 ** 20
 FRONT_VMEM = 48 * MIB
 ATTEND_VMEM = 46 * MIB
-TAIL_VMEM = 50 * MIB
+TAIL_VMEM = 48 * MIB
 SEND_ORDER = (2, 1, 3)
 WAIT_ORDER = (1, 3, 2)
 MESH = pl.DeviceIdType.MESH
@@ -44,7 +44,7 @@
 
 
 def front_kernel(hid_ref, gq_ref, gkv_ref, cos_ref, sin_ref, wdkv_hbm, wdq_hbm, wuk_hbm, wuq_hbm,
-                 qabs_ref, qrope_ref, lnew_ref, rnew_ref, wdkv_v, wdq_v, wuk_v, wuq_v, sem_kv, sem_q, sem_k, sem_u):
+                 qabs_ref, qrope_ref, lnew_ref, rnew_ref, wdkv_v, wdq_v, wuk_v, wuq_v, wk_v, nope_v, turn_v, ab_v, sem_kv, sem_q, sem_k, sem_u):
     n_kv, n_q, ring = wdkv_v.shape[0], wdq_v.shape[0], wuq_v.shape[0]
     kv_cols, q_rows, part = wdkv_v.shape[2], wdq_v.shape[1], wuq_v.shape[1]
     n_parts = wuq_hbm.shape[0] // part
@@ -57,7 +57,7 @@
     k_rows = wuk_v.shape[0] // 4
     k_loads = [pltpu.make_async_copy(wuk_hbm.at[pl.ds(i * k_rows, k_rows)], wuk_v.at[pl.ds(i * k_rows, k_rows)], sem_k.at[i]) for i in range(4)]
     uq_loads = [load_uq(i) for i in range(n_parts)]
-    queue = kv_loads + q_loads + uq_loads[:2] + k_loads + uq_loads[2:]
+    queue = k_loads + kv_loads + q_loads + uq_loads
     state = [0]
 
     def issue(count):
@@ -76,8 +76,11 @@
     def norm(values, gain_ref):
         v = values.astype(bf16).astype(f32)
         inv = lax.rsqrt(jnp.mean(v * v, axis=1, keepdims=True) + EPSILON)
-        return (v * inv * gain_ref[...].astype(f32)).astype(bf16)
-
+        return (v * inv * gain_ref[...].astype(f32)[None, :]).astype(bf16)
+
+    for copy in k_loads:
+        copy.wait()
+        issue(1)
     kv = jnp.zeros((32, wdkv_v.shape[1]), f32)
     for i in range(n_kv):
         kv_loads[i].wait()
@@ -94,37 +97,29 @@
         h_q = h_q + jnp.dot(hid_ref[:, i * q_rows:(i + 1) * q_rows], wdq_v[i], preferred_element_type=f32)
     cq = norm(h_q, gq_ref)
 
-    nope, rotated = [], []
     zero = jnp.zeros((32, 128), bf16)
-
-    def absorb(group):
-        wuk = jnp.swapaxes(wuk_v[:, group * HEAD_GROUP:(group + 1) * HEAD_GROUP, :], 0, 1)
-        absorbed = []
-        for i in range(0, HEAD_GROUP, 2):
-            a, b = nope[group * HEAD_GROUP + i], nope[group * HEAD_GROUP + i + 1]
-            pair = jnp.concatenate([jnp.concatenate([a, zero], axis=1), jnp.concatenate([zero, b], axis=1)], axis=0)
-            both = lax.dot_general(pair, jnp.concatenate([wuk[i], wuk[i + 1]], axis=1), NT, preferred_element_type=f32)
-            absorbed += [both[:32], both[32:]]
-        where = slice(group * HEAD_GROUP, (group + 1) * HEAD_GROUP)
-        qabs_ref[:, where, :] = jnp.swapaxes(jnp.stack(absorbed), 0, 1).astype(bf16)
-        qrope_ref[:, where, :] = jnp.swapaxes(jnp.stack(rotated[where]), 0, 1).astype(bf16)
-
     per_group = HEAD_GROUP // part
     for i in range(n_parts):
+        heads = slice(i // per_group * HEAD_GROUP, (i // per_group + 1) * HEAD_GROUP)
+        first = i % per_group * part
+        if first == 0:
+            wk_v[...] = jnp.swapaxes(wuk_v[:, heads, :], 0, 1)
         uq_loads[i].wait()
         w = wuq_v[i % ring].reshape(part * 192, 1536)
         q4 = lax.dot_general(cq, w, NT, preferred_element_type=f32).astype(bf16)
+        issue(1)
         for j in range(part):
             q = q4[:, j * 192:j * 192 + 192]
-            nope.append(q[:, :128])
-            rotated.append(rotate(q[:, 128:].astype(f32)))
-        issue(1)
-        if i == 1:
-            for copy in k_loads:
-                copy.wait()
-                issue(1)
-        if i % per_group == per_group - 1:
-            absorb(i // per_group)
+            nope_v[first + j] = q[:, :128]
+            turn_v[first + j] = rotate(q[:, 128:].astype(f32))
+        for j in range(first, first + part, 2):
+            k = j + 1
+            pair = jnp.concatenate([jnp.concatenate([nope_v[j], zero], axis=1), jnp.concatenate([zero, nope_v[k]], axis=1)], axis=0)
+            both = lax.dot_general(pair, jnp.concatenate([wk_v[j], wk_v[k]], axis=1), NT, preferred_element_type=f32)
+            ab_v[j], ab_v[k] = both[:32], both[32:]
+        if first + part == HEAD_GROUP:
+            qabs_ref[:, heads, :] = jnp.swapaxes(ab_v[...], 0, 1).astype(bf16)
+            qrope_ref[:, heads, :] = jnp.swapaxes(turn_v[...], 0, 1).astype(bf16)
 
 
 def front(hidden, gain_q, gain_kv, cos_t, sin_t, w_dkv, w_dq, w_uk, w_uq):
@@ -139,15 +134,19 @@
         in_specs=[vmem] * 5 + [hbm] * 4,
         out_specs=[vmem] * 4,
         scratch_shapes=[
-            pltpu.VMEM((4, 576, 1280), bf16),
+            pltpu.VMEM((UQ_RING, 576, 1280), bf16),
             pltpu.VMEM((5, 1024, 1536), bf16),
             pltpu.VMEM((512, heads, 128), bf16),
             pltpu.VMEM((UQ_RING, 4, 192, 1536), bf16),
-            dma((4,)), dma((5,)), dma((4,)), dma((UQ_RING,)),
+            pltpu.VMEM((HEAD_GROUP, 512, 128), bf16),
+            pltpu.VMEM((HEAD_GROUP, 32, 128), bf16),
+            pltpu.VMEM((HEAD_GROUP, 32, 64), f32),
+            pltpu.VMEM((HEAD_GROUP, 32, 512), f32),
+            dma((UQ_RING,)), dma((5,)), dma((UQ_RING,)), dma((UQ_RING,)),
         ],
         compiler_params=pltpu.CompilerParams(vmem_limit_bytes=FRONT_VMEM),
         name='front',
-    )(hidden, gain_q.reshape(1, -1), gain_kv.reshape(1, -1), cos_t, sin_t, w_dkv.T, w_dq, w_uk, w_uq.transpose(1, 2, 0))
+    )(hidden, gain_q, gain_kv, cos_t, sin_t, w_dkv.T, w_dq, w_uk, w_uq.transpose(1, 2, 0))
 
 
 def attend_kernel(base_ref, pos_ref, qabs_ref, qrope_ref, lat_ref, rope_ref, lnew_ref, rnew_ref,
@@ -389,13 +388,15 @@
         [jnp.concatenate([units[bt * 4 + kt] for kt in range(4)], axis=1) for bt in range(4)], axis=0).astype(jnp.bfloat16)
     o_head = jnp.dot(o_lat, wuv_h[...], preferred_element_type=jnp.float32).astype(jnp.bfloat16)
     load_out.wait()
-    for half in range(2):
+    def project(half):
         for cg in range(4):
-            base = half * 2560 + cg * 640
-            part = jnp.dot(o_head, wout_v[:, base:base + 640], preferred_element_type=jnp.float32)
+            columns = pl.ds(pl.multiple_of((half * 4 + cg) * 640, 128), 640)
+            part = jnp.dot(o_head, wout_v[:, columns], preferred_element_type=f32)
             y_buf[half, :, cg] = part.reshape(4, 8, 640)
 
+    project(1 - tp)
     pair = send(y_buf.at[1 - tp], y_in, {'tp': 1 - tp})
+    project(tp)
     pair.wait_recv()
     y_in[...] = y_in[...] + y_buf[tp]
 
@@ -445,20 +446,24 @@
         mine = g_buf.at[tp, x, :, :, cols] if axis == 0 else g_buf.at[tp, :, y, :, cols]
         for step in SEND_ORDER:
             pending[colour, step] = send(mine, mine, peer_id(axis, step))
+    pairs = []
     for colour in range(2):
+        cols = pl.ds(OUT_LO[colour], OUT_HI[colour] - OUT_LO[colour])
         for step in WAIT_ORDER:
             pending[colour, step].wait_recv()
-    pair = send(g_buf.at[tp], g_buf.at[tp], {'tp': 1 - tp})
-    pair.wait_recv()
+        mine = g_buf.at[tp, :, :, :, cols]
+        pairs.append(send(mine, mine, {'tp': 1 - tp}))
+    for pair in pairs:
+        pair.wait_recv()
     for half in range(2):
         for cg in range(4):
-            base = half * 2560 + cg * 640
+            base = (half * 4 + cg) * 640
             out_ref[:, base:base + 640] = g_buf[half, :, cg].reshape(32, 640)
     for copy in started:
         copy.wait_send()
 
 
-N_SENDS = 95
+N_SENDS = 96
 
 
 def tail(u_parts, stats, w_uv, w_out):

time: 107 us -> 104 us (0.972)
  local copies, waits for them, and re-layouts: 4.3 us -> 2.34 us
    pallas_call x1, Pallas kernels: 59.7 us -> 57.9 us  [tail(): pl.pallas_call(tail_kernel, out_shape=jax.ShapeDtypeStruct((32, 5120), f3...]
    reshape x2 -> x0, local copies, waits for them, and re-layouts: 1.38 us -> none  [the longest x1 0.69 us: front(): gain_q.reshape(1, -1)]
    unnamed x10 -> x12, local copies, waits for them, and re-layouts: 2.92 us -> 2.34 us
where the time goes in v1:
time: 104 us
  Pallas kernels  99.6 us (96%)
  local copies, waits for them, and re-layouts  2.34 us (2%)
  other arithmetic  1.59 us (2%)
    pallas_call x1, Pallas kernels, tail(): pl.pallas_call(tail_kernel, out_shape=jax.ShapeDtypeStruct((32, 5120), f3...  57.9 us
    pallas_call x1, Pallas kernels, front(): pl.pallas_call(front_kernel, out_shape=(shape((32, heads, 512), bf16), sh...  33.2 us
    pallas_call x1, Pallas kernels, attend(): pl.pallas_call(functools.partial(attend_kernel, scale=scale), grid=(4,),...  8.48 us
    unnamed x12, local copies, waits for them, and re-layouts  2.34 us

profile of v1, /device:TPU:1, one launch (start us, length us, event | category | flops | bytes accessed | tf_op | source)
XLA Modules:
  0.0 104.2 jit_solution(10161431408225966935)
XLA Ops:
  0.6 0.7 convert_element_type.17
  1.3 0.1 multiply_sine_fusion
  1.5 0.0 copy-start
  1.5 1.0 copy-done
  2.4 0.0 copy-start.3
  2.4 0.7 copy-done.3
  3.1 0.0 copy-start.4
  3.1 0.7 copy-done.4
  3.8 0.0 copy-start.2
  3.8 0.0 copy-start.5
  3.8 33.2 %front.1 = (bf16[32,64,512]{2,1,0:T(8,128)(2,1)S(1)}, bf16[32,64,64]{2,1,0:T(8,128)(2,1)S(1)}, bf16[32,512]{1,0:T(8,128)(2,1)S(1)}, bf16[4,64,8]{2,1,0:T(8,128)(2,1)S(1)}) custom-call(bf16[32,5120]{1,0:T(8,128)(2,1)S(1)} %copy-done, bf16[1536]{0:T(1024)(128)(2,1)S(1)} %copy-done.3, bf16[512]{0:T(512)(128)(2,1)S(1)} %copy-done.4, ...), custom_call_target="tpu_custom_call" | custom-call | tf_op jit(solution)/shard_map/front/pallas_call | solution.py:131
  37.0 0.0 copy-done.2
  37.0 0.0 copy-done.5
  37.0 8.5 %attend.1 = (bf16[32,256,512]{2,1,0:T(8,128)(2,1)}, bf16[32,64,256]{2,1,0:T(8,128)(2,1)}, f32[16,512,128]{2,1,0:T(8,128)S(1)}, f32[4,8,128]{2,1,0:T(8,128)S(1)}) custom-call(s32[1]{0:T(128)} %bitcast.base_ref, s32[32]{0:T(128)S(1)} %copy-done.5, bf16[32,64,512]{2,1,0:T(8,128)(2,1)S(1)} %get-tuple-element.11.qabs_ref, ...), custom_call_target="tpu_custom_call" | custom-call | tf_op jit(solution)/shard_map/attend/pallas_call | solution.py:192
  45.5 0.0 copy-start.1
  45.5 57.9 %tail.1 = f32[32,5120]{1,0:T(8,128)S(1)} custom-call(f32[16,4,4,4,8,128]{5,4,3,2,1,0:T(8,128)S(1)} %bitcast.6, f32[4,8,128]{2,1,0:T(8,128)S(1)} %get-tuple-element.16.st_ref, bf16[512,64,128]{2,1,0:T(8,128)(2,1)} %wuv_ref.1, bf16[8192,5120]{1,0:T(8,128)(2,1)} %wout_ref.1), custom_call_target="tpu_custom_call" | custom-call | tf_op jit(solution)/shard_map/tail/pallas_call | solution.py:475
  103.4 0.0 copy-done.1
  103.4 0.8 add_convert_fusion
  (1 shorter events, 0.0 us)
Async XLA Ops:
  1.5 1.0 copy-start
  2.4 0.7 copy-start.3
  3.1 0.7 copy-start.4
  3.8 33.2 %copy-start.2 = (bf16[32,256,64]{1,2,0:T(8,128)(2,1)S(1)}, bf16[32,256,64]{1,2,0:T(8,128)(2,1)}, u32[]{:S(2)}) copy-start(bf16[32,256,64]{1,2,0:T(8,128)(2,1)} %param.14) | copy-start | bytes 3145732
  3.8 33.2 %copy-start.5 = (s32[32]{0:T(128)S(1)}, s32[32]{0:T(128)}, u32[]{:S(2)}) copy-start(s32[32]{0:T(128)} %pos_ref.1) | copy-start | bytes 388
  45.5 57.9 %copy-start.1 = (bf16[32,5120]{1,0:T(8,128)(2,1)S(1)}, bf16[32,5120]{1,0:T(8,128)(2,1)}, u32[]{:S(2)}) copy-start(bf16[32,5120]{1,0:T(8,128)(2,1)} %hid_ref.1) | copy-start | bytes 983044

commit v2 on v1

--- a/solution.py
+++ b/solution.py
@@ -39,11 +39,11 @@
 def rope_tables(positions, rope_dim):
     half_dim = rope_dim // 2
     inv_freq = ROPE_BASE ** (-jnp.arange(half_dim).astype(jnp.float32) / half_dim)
-    angles = positions.astype(jnp.float32)[:, None] * inv_freq[None, :]
+    angles = positions.astype(f32)[:, None] * inv_freq[None, :]
     return jnp.cos(angles), jnp.sin(angles)
 
 
-def front_kernel(hid_ref, gq_ref, gkv_ref, cos_ref, sin_ref, wdkv_hbm, wdq_hbm, wuk_hbm, wuq_hbm,
+def front_kernel(hid_ref, gain_ref, cos_ref, sin_ref, wdkv_hbm, wdq_hbm, wuk_hbm, wuq_hbm,
                  qabs_ref, qrope_ref, lnew_ref, rnew_ref, wdkv_v, wdq_v, wuk_v, wuq_v, wk_v, nope_v, turn_v, ab_v, sem_kv, sem_q, sem_k, sem_u):
     n_kv, n_q, ring = wdkv_v.shape[0], wdq_v.shape[0], wuq_v.shape[0]
     kv_cols, q_rows, part = wdkv_v.shape[2], wdq_v.shape[1], wuq_v.shape[1]
@@ -57,7 +57,7 @@
     k_rows = wuk_v.shape[0] // 4
     k_loads = [pltpu.make_async_copy(wuk_hbm.at[pl.ds(i * k_rows, k_rows)], wuk_v.at[pl.ds(i * k_rows, k_rows)], sem_k.at[i]) for i in range(4)]
     uq_loads = [load_uq(i) for i in range(n_parts)]
-    queue = k_loads + kv_loads + q_loads + uq_loads
+    queue = kv_loads + q_loads + k_loads + uq_loads
     state = [0]
 
     def issue(count):
@@ -73,20 +73,17 @@
         v1, v2 = v[:, :half], v[:, half:]
         return jnp.concatenate([v1 * cos_t - v2 * sin_t, v2 * cos_t + v1 * sin_t], axis=1)
 
-    def norm(values, gain_ref):
+    def norm(values, gain):
         v = values.astype(bf16).astype(f32)
         inv = lax.rsqrt(jnp.mean(v * v, axis=1, keepdims=True) + EPSILON)
-        return (v * inv * gain_ref[...].astype(f32)[None, :]).astype(bf16)
-
-    for copy in k_loads:
-        copy.wait()
-        issue(1)
+        return (v * inv * gain.astype(f32)[None, :]).astype(bf16)
+
     kv = jnp.zeros((32, wdkv_v.shape[1]), f32)
     for i in range(n_kv):
         kv_loads[i].wait()
         issue(1)
         kv = kv + lax.dot_general(hid_ref[:, i * kv_cols:(i + 1) * kv_cols], wdkv_v[i], NT, preferred_element_type=f32)
-    lnew_ref[...] = norm(kv[:, :512], gkv_ref)
+    lnew_ref[...] = norm(kv[:, :512], gain_ref[1536:])
     turned = rotate(kv[:, 512:].astype(bf16).astype(f32)).T.astype(bf16)
     for t in range(4):
         rnew_ref[t] = turned[:, t * 8:t * 8 + 8]
@@ -95,7 +92,10 @@
         q_loads[i].wait()
         issue(1)
         h_q = h_q + jnp.dot(hid_ref[:, i * q_rows:(i + 1) * q_rows], wdq_v[i], preferred_element_type=f32)
-    cq = norm(h_q, gq_ref)
+    cq = norm(h_q, gain_ref[:1536])
+    for copy in k_loads:
+        copy.wait()
+        issue(1)
 
     zero = jnp.zeros((32, 128), bf16)
     per_group = HEAD_GROUP // part
@@ -131,7 +131,7 @@
     return pl.pallas_call(
         front_kernel,
         out_shape=(shape((32, heads, 512), bf16), shape((32, heads, 64), bf16), shape((32, 512), bf16), shape((4, 64, 8), bf16)),
-        in_specs=[vmem] * 5 + [hbm] * 4,
+        in_specs=[vmem] * 4 + [hbm] * 4,
         out_specs=[vmem] * 4,
         scratch_shapes=[
             pltpu.VMEM((UQ_RING, 576, 1280), bf16),
@@ -146,7 +146,7 @@
         ],
         compiler_params=pltpu.CompilerParams(vmem_limit_bytes=FRONT_VMEM),
         name='front',
-    )(hidden, gain_q, gain_kv, cos_t, sin_t, w_dkv.T, w_dq, w_uk, w_uq.transpose(1, 2, 0))
+    )(hidden, jnp.concatenate([gain_q, gain_kv]), cos_t, sin_t, w_dkv.T, w_dq, w_uk, w_uq.transpose(1, 2, 0))
 
 
 def attend_kernel(base_ref, pos_ref, qabs_ref, qrope_ref, lat_ref, rope_ref, lnew_ref, rnew_ref,

time: 104 us -> 103 us (level)
  local copies, waits for them, and re-layouts: 2.34 us -> 0.98 us
    unnamed x12 -> x8, local copies, waits for them, and re-layouts: 2.34 us -> 0.98 us
where the time goes in v2:
time: 103 us
  Pallas kernels  98.8 us (96%)
  other arithmetic  2.3 us (2%)
    pallas_call x1, Pallas kernels, tail(): pl.pallas_call(tail_kernel, out_shape=jax.ShapeDtypeStruct((32, 5120), f3...  57.9 us
    pallas_call x1, Pallas kernels, front(): pl.pallas_call(front_kernel, out_shape=(shape((32, heads, 512), bf16), sh...  32.4 us
    pallas_call x1, Pallas kernels, attend(): pl.pallas_call(functools.partial(attend_kernel, scale=scale), grid=(4,),...  8.51 us

profile of v2, /device:TPU:1, one launch (start us, length us, event | category | flops | bytes accessed | tf_op | source)
XLA Modules:
  0.0 102.8 jit_solution(714560858628264554)
XLA Ops:
  0.6 0.7 convert_element_type.17
  1.3 0.7 pad_maximum_fusion.gain_ref
  2.0 0.1 multiply_sine_fusion
  2.2 0.0 copy-start
  2.2 1.0 copy-done
  3.1 0.0 copy-start.2
  3.1 0.0 copy-start.3
  3.1 32.4 %front.1 = (bf16[32,64,512]{2,1,0:T(8,128)(2,1)S(1)}, bf16[32,64,64]{2,1,0:T(8,128)(2,1)S(1)}, bf16[32,512]{1,0:T(8,128)(2,1)S(1)}, bf16[4,64,8]{2,1,0:T(8,128)(2,1)S(1)}) custom-call(bf16[32,5120]{1,0:T(8,128)(2,1)S(1)} %copy-done, bf16[2048]{0:T(1024)(128)(2,1)S(1)} %pad_maximum_fusion.gain_ref, f32[32,32]{1,0:T(8,128)S(1)} %get-tuple-element.20.cos_ref, ...), custom_call_target="tpu_custom_call" | custom-call | tf_op jit(solution)/shard_map/front/pallas_call | solution.py:131
  35.6 0.0 copy-done.2
  35.6 0.0 copy-done.3
  35.6 8.5 %attend.1 = (bf16[32,256,512]{2,1,0:T(8,128)(2,1)}, bf16[32,64,256]{2,1,0:T(8,128)(2,1)}, f32[16,512,128]{2,1,0:T(8,128)S(1)}, f32[4,8,128]{2,1,0:T(8,128)S(1)}) custom-call(s32[1]{0:T(128)} %bitcast.base_ref, s32[32]{0:T(128)S(1)} %copy-done.3, bf16[32,64,512]{2,1,0:T(8,128)(2,1)S(1)} %get-tuple-element.11.qabs_ref, ...), custom_call_target="tpu_custom_call" | custom-call | tf_op jit(solution)/shard_map/attend/pallas_call | solution.py:192
  44.1 0.0 copy-start.1
  44.1 57.9 %tail.1 = f32[32,5120]{1,0:T(8,128)S(1)} custom-call(f32[16,4,4,4,8,128]{5,4,3,2,1,0:T(8,128)S(1)} %bitcast.6, f32[4,8,128]{2,1,0:T(8,128)S(1)} %get-tuple-element.16.st_ref, bf16[512,64,128]{2,1,0:T(8,128)(2,1)} %wuv_ref.1, bf16[8192,5120]{1,0:T(8,128)(2,1)} %wout_ref.1), custom_call_target="tpu_custom_call" | custom-call | tf_op jit(solution)/shard_map/tail/pallas_call | solution.py:475
  102.0 0.0 copy-done.1
  102.0 0.8 add_convert_fusion
  (1 shorter events, 0.0 us)
Async XLA Ops:
  2.2 1.0 copy-start
  3.1 32.4 %copy-start.2 = (bf16[32,256,64]{1,2,0:T(8,128)(2,1)S(1)}, bf16[32,256,64]{1,2,0:T(8,128)(2,1)}, u32[]{:S(2)}) copy-start(bf16[32,256,64]{1,2,0:T(8,128)(2,1)} %param.14) | copy-start | bytes 3145732
  3.1 32.4 %copy-start.3 = (s32[32]{0:T(128)S(1)}, s32[32]{0:T(128)}, u32[]{:S(2)}) copy-start(s32[32]{0:T(128)} %pos_ref.1) | copy-start | bytes 388
  44.1 57.9 %copy-start.1 = (bf16[32,5120]{1,0:T(8,128)(2,1)S(1)}, bf16[32,5120]{1,0:T(8,128)(2,1)}, u32[]{:S(2)}) copy-start(bf16[32,5120]{1,0:T(8,128)(2,1)} %hid_ref.1) | copy-start | bytes 983044
